TPU v7x, 32 devices: a whole 2x2x4 slice. The times are simulated.
32 devices in a mesh: row: 4 (over y, core), col: 8 (over z, x).
Axes of the slice: x: 2, y: 2, z: 4, core: 2. Of those that a mesh axis runs over, the one named last changes fastest.
Arguments:
- l_saved: bfloat16 [16, 4, 256, 8, 256], P(None, 'row', None, 'col'), as said below
- l_grad: bfloat16 [16, 4, 256, 8, 256], P(None, 'row', None, 'col'), as said below
Outputs:
- grad_out: float32 [16, 4, 256, 8, 256], P(None, 'row', None, 'col')
Inputs may be any that keep to these rules, and one draw needn't show every extreme that they name: Read as one matrix of 16384 rows, l_saved is lower triangular with its diagonal between 1 and 2. Read as one matrix, l_grad is zero above the diagonal.
All inputs are finite; a program needn't handle non-finite values.
Results may differ from a plain program's by a relative error of at most 0.0003.
Values may be sent and summed in bfloat16 or wider, within the bound.
A program may use at most 64 MiB of HBM per device.

v0:
```python
import jax
import jax.numpy as jnp
from jax import lax
from jax.sharding import PartitionSpec as P

HIGH = lax.Precision.HIGHEST


def from_root(array, axis, root):
    mine = lax.axis_index(axis) == root
    return lax.psum(jnp.where(mine, array, jnp.zeros_like(array)), axis)


def right_solve(factor, rhs):
    return lax.linalg.triangular_solve(factor, rhs, left_side=False, lower=True)


def diag_gradient(factor, lower_part):
    eye = jnp.eye(factor.shape[0], dtype=jnp.float32)
    middle = jnp.dot(factor.T, lower_part, precision=HIGH, preferred_element_type=jnp.float32)
    middle = jnp.tril(middle) - 0.5 * middle * eye
    half = lax.linalg.triangular_solve(factor, middle, left_side=True, lower=True, transpose_a=True)
    full = right_solve(factor, half)
    return full + full.T


def stacked_inner(left, right):
    flat_left = left.reshape(-1, left.shape[-1])
    flat_right = right.reshape(-1, right.shape[-1]).astype(jnp.float32)
    return lax.dot_general(
        flat_left,
        flat_right,
        (((0,), (0,)), ((), ())),
        precision=HIGH,
        preferred_element_type=jnp.float32,
    )


def solve_rows(diag_factor, column, below):
    rows_here, tile = (column.shape[0], column.shape[1])
    inverse = right_solve(diag_factor, jnp.eye(tile, dtype=jnp.float32))
    solved = jnp.dot(
        column.reshape(-1, tile), inverse, precision=HIGH, preferred_element_type=jnp.float32
    ).reshape(rows_here, tile, tile)
    return jnp.where(below, solved, jnp.float32(0.0))


def diag_down(piece, owner_row):
    return from_root(piece, "row", owner_row).astype(jnp.float32)


def per_device(l_saved, l_grad):
    rows_here = l_saved.shape[0]
    tile = l_saved.shape[2]
    n_row = lax.axis_size("row")
    n_col = lax.axis_size("col")
    factor = l_saved.reshape(rows_here, tile, tile)
    grad = l_grad.reshape(rows_here, tile, tile).astype(jnp.float32)
    my_row = lax.axis_index("row")
    my_col = lax.axis_index("col")
    tile_rows = jnp.arange(rows_here, dtype=jnp.int32) * n_row + my_row
    eye = jnp.eye(tile, dtype=jnp.float32)
    for panel in (n_col - 1, n_col - 2):
        owner_row = panel % n_row
        local = panel // n_row
        at_owner = my_row == owner_row
        below = (tile_rows > panel)[:, None, None]
        diag_factor = diag_down(factor[local], owner_row)
        cbar = solve_rows(diag_factor, grad, below)
        term = jnp.where(at_owner, grad[local], jnp.float32(0.0)) - stacked_inner(cbar, factor)
        total = lax.psum(term, "row")
        sym = diag_gradient(diag_factor, jnp.tril(total))
        sent = from_root(jnp.concatenate([cbar, sym[None]], 0), "col", panel)
        cbar = sent[:rows_here]
        sym = sent[rows_here]
        row_factor = from_root(factor[local], "row", owner_row).astype(jnp.float32)
        update = jnp.dot(
            cbar.reshape(-1, tile), row_factor, precision=HIGH, preferred_element_type=jnp.float32
        )
        partial_sum = stacked_inner(cbar, factor)
        summed = lax.psum(partial_sum, "row")
        own_row = grad[local] - (
            summed + jnp.dot(sym, row_factor, precision=HIGH, preferred_element_type=jnp.float32)
        )
        updated = grad - update.reshape(rows_here, tile, tile)
        updated = updated.at[local].set(jnp.where(at_owner, own_row, updated[local]))
        abar = jnp.tril(sym) - 0.5 * sym * eye
        panel_col = jnp.where(
            below,
            cbar,
            jnp.where((tile_rows == panel)[:, None, None], abar[None], jnp.float32(0.0)),
        )
        grad = jnp.where(my_col < panel, updated, jnp.where(my_col == panel, panel_col, grad))
    return grad.reshape(l_grad.shape)


def solution(mesh):
    in_specs = (P(None, "row", None, "col", None), P(None, "row", None, "col", None))
    out_specs = P(None, "row", None, "col", None)
    return jax.shard_map(
        per_device, mesh=mesh, in_specs=in_specs, out_specs=out_specs, check_vma=False
    )
```

profile of v0, /device:TPU:0, one launch (start us, length us, event | category | flops | bytes accessed | tf_op | source)
XLA Modules:
  0.0 607.6 jit_solution(4179768059537039904)
XLA Ops:
  6.5 1.6 select_bitcast_fusion.1
  8.3 4.3 convert_element_type.13
  12.6 32.2 %all-reduce.21.cloned.1.call-done = (bf16[256,256]{1,0:T(8,128)(2,1)}, bf16[256,256]{1,0:T(8,128)(2,1)}) async-done(((bf16[256,256]{1,0:T(8,128)(2,1)}, bf16[256,256]{1,0:T(8,128)(2,1)}), (bf16[256,256]{1,0:T(8,128)(2,1)}, bf16[256,256]{1,0:T(8,128)(2,1)})) %all-reduce.21.cloned.1.call-update) | async-done | bytes 262160 | tf_op jit(solution)/shard_map/psum | solution.py:11
  44.8 1.0 fusion.25
  45.9 4.1 while.14
  46.0 0.6 fusion.114
  46.6 1.4 bitcast_dynamic-update-slice_fusion.4
  48.0 0.6 fusion.114
  48.6 1.4 bitcast_dynamic-update-slice_fusion.4
  50.1 19.7 %custom-call.10 = f32[2,128,128]{1,2,0:T(8,128)S(1)} custom-call(f32[2,128,128]{2,1,0:T(8,128)S(1)} %get-tuple-element.71), custom_call_target="InvertDiagBlocksLowerTriangular" | custom-call | tf_op jit(solution)/shard_map/triangular_solve/custom-call.1 | solution.py:15
  69.7 0.3 fusion.60
  70.0 0.4 convolution_subtract_fusion.7
  70.4 0.3 fusion.64
  70.7 3.8 convolution_bitcast_fusion
  74.6 5.8 copy.9
  80.3 5.0 fusion.5
  85.4 4.7 broadcast_select_fusion
  90.2 27.7 %all-reduce.9.cloned.1.call-done = f32[256,256]{1,0:T(8,128)} async-done(((f32[256,256]{1,0:T(8,128)}), f32[256,256]{1,0:T(8,128)}) %all-reduce.9.cloned.1.call-update) | async-done | bytes 262160 | tf_op jit(solution)/shard_map/psum | solution.py:71
  117.9 1.3 fusion.33
  119.4 0.3 convolution_subtract_fusion.6
  120.0 0.3 fusion.50
  120.3 0.4 convolution_subtract_fusion.5
  120.7 0.3 fusion.62
  120.9 0.7 pad_maximum_fusion
  121.7 1.1 copy.4
  122.8 4.7 maximum_select_fusion
  127.5 13.2 %all-reduce.13.cloned.1.call-start = ((), (), s32[]{:S(2)}) async-start(), calls=%async_computation.2 | async-start | bytes 524288 | tf_op jit(solution)/shard_map/psum | solution.py:81
  140.7 4.0 while.15
  140.7 0.6 fusion.115
  141.3 1.4 bitcast_dynamic-update-slice_fusion.5
  142.7 0.6 fusion.115
  143.3 1.4 bitcast_dynamic-update-slice_fusion.5
  144.7 19.7 %custom-call.13 = f32[2,128,128]{1,2,0:T(8,128)S(1)} custom-call(f32[2,128,128]{2,1,0:T(8,128)S(1)} %get-tuple-element.74), custom_call_target="InvertDiagBlocksLowerTriangular" | custom-call | tf_op jit(solution)/shard_map/triangular_solve/custom-call.1 | solution.py:15
  164.4 0.3 fusion.58
  164.7 0.4 convolution_subtract_fusion.4
  165.1 0.3 fusion.67
  165.3 125.3 %all-reduce.11.cloned.1.call-done = f32[17,256,256]{2,1,0:T(8,128)} async-done(((f32[17,256,256]{2,1,0:T(8,128)}), f32[17,256,256]{2,1,0:T(8,128)}) %all-reduce.11.cloned.1.call-update) | async-done | bytes 4456464 | tf_op jit(solution)/shard_map/psum | solution.py:11
  290.7 2.2 slice-done.3
  292.9 4.1 fusion.83
  297.1 4.9 bitcast_subtract_fusion
  302.0 2.0 copy-done.5
  304.0 1.0 subtract_bitcast_fusion.1
  305.0 23.4 %all-reduce.13.cloned.1.call-done = f32[256,256]{1,0:T(8,128)} async-done(((f32[256,256]{1,0:T(8,128)}), f32[256,256]{1,0:T(8,128)}) %all-reduce.13.cloned.1.call-update) | async-done | bytes 262160 | tf_op jit(solution)/shard_map/psum | solution.py:81
  328.5 2.1 fusion.12
  330.5 5.1 fusion
  335.7 3.7 convolution_select_fusion
  339.4 1.9 copy-done.1
  341.3 4.2 convolution_subtract_fusion.1
  345.6 31.5 %all-reduce.15.cloned.1.call-done = f32[256,256]{1,0:T(8,128)} async-done(((f32[256,256]{1,0:T(8,128)}), f32[256,256]{1,0:T(8,128)}) %all-reduce.15.cloned.1.call-update) | async-done | bytes 262160 | tf_op jit(solution)/shard_map/psum | solution.py:71
  377.1 1.3 fusion.36
  378.6 0.3 convolution_subtract_fusion.3
  379.2 0.3 fusion.46
  379.5 0.4 convolution_subtract_fusion.2
  379.9 0.3 fusion.65
  380.3 4.7 maximum_select_fusion.1
  385.3 162.9 %all-reduce.17.cloned.1.call-done = f32[17,256,256]{2,1,0:T(8,128)} async-done(((f32[17,256,256]{2,1,0:T(8,128)}), f32[17,256,256]{2,1,0:T(8,128)}) %all-reduce.17.cloned.1.call-update) | async-done | bytes 4456464 | tf_op jit(solution)/shard_map/psum | solution.py:11
  548.2 2.2 slice-done.2
  550.4 4.1 fusion.84
  554.6 5.6 convolution_subtract_fusion
  560.2 2.0 copy-done.4
  562.3 23.7 %all-reduce.19.cloned.1.call-done = f32[256,256]{1,0:T(8,128)} async-done(((f32[256,256]{1,0:T(8,128)}), f32[256,256]{1,0:T(8,128)}) %all-reduce.19.cloned.1.call-update) | async-done | bytes 262160 | tf_op jit(solution)/shard_map/psum | solution.py:81
  586.0 2.1 fusion.15
  588.1 5.9 select_bitcast_fusion
  594.0 6.3 %copy.7 = f32[16,1,256,1,256]{4,3,2,1,0:T(1,128)} copy(f32[16,1,256,1,256]{4,2,0,3,1:T(8,128)S(1)} %select_bitcast_fusion) | data formatting | bytes 8388608 | tf_op jit(solution)/shard_map/reshape | solution.py:94
  (58 shorter events, 2.1 us)
Async XLA Ops:
  6.5 38.3 %all-reduce.21.cloned.1.call-start = ((), (), s32[]{:S(2)}) async-start(), calls=%async_computation.6 | async-start | bytes 524288 | tf_op jit(solution)/shard_map/psum | solution.py:11
  8.2 109.7 %all-reduce.9.cloned.1.call-start = ((), (), s32[]{:S(2)}) async-start(), calls=%async_computation | async-start | bytes 524288 | tf_op jit(solution)/shard_map/psum | solution.py:71
  8.3 62.4 %copy-start.3 = (bf16[16,1,256,1,256]{4,2,3,1,0:T(8,128)(2,1)S(1)}, bf16[16,1,256,1,256]{4,2,3,1,0:T(8,128)(2,1)}, u32[]{:S(2)}) copy-start(bf16[16,1,256,1,256]{4,2,3,1,0:T(8,128)(2,1)} %param.11) | copy-start | bytes 6291460
  74.6 5.8 copy-start.2
  85.4 205.3 %all-reduce.11.cloned.1.call-start = ((), (), s32[]{:S(2)}) async-start(), calls=%async_computation.1 | async-start | bytes 8912896 | tf_op jit(solution)/shard_map/psum | solution.py:11
  85.4 32.4 %copy-start.7 = (bf16[256,256]{1,0:T(8,128)(2,1)S(1)}, bf16[256,256]{1,0:T(8,128)(2,1)}, u32[]{:S(2)}) copy-start(bf16[256,256]{1,0:T(8,128)(2,1)} %get-tuple-element.93) | copy-start | bytes 393220
  127.5 201.0 %all-reduce.13.cloned.1.call-start = ((), (), s32[]{:S(2)}) async-start(), calls=%async_computation.2 | async-start | bytes 524288 | tf_op jit(solution)/shard_map/psum | solution.py:81
  290.7 2.2 slice-start.3
  297.0 80.1 %all-reduce.15.cloned.1.call-start = ((), (), s32[]{:S(2)}) async-start(), calls=%async_computation.3 | async-start | bytes 524288 | tf_op jit(solution)/shard_map/psum | solution.py:71
  302.0 2.0 copy-start.5
  335.6 3.8 copy-start
  339.4 1.9 copy-start.1
  339.4 37.7 %copy-start.6 = (bf16[256,256]{1,0:T(8,128)(2,1)S(1)}, bf16[256,256]{1,0:T(8,128)(2,1)}, u32[]{:S(2)}) copy-start(bf16[256,256]{1,0:T(8,128)(2,1)} %get-tuple-element.94) | copy-start | bytes 393220
  345.5 202.7 %all-reduce.17.cloned.1.call-start = ((), (), s32[]{:S(2)}) async-start(), calls=%async_computation.4 | async-start | bytes 8912896 | tf_op jit(solution)/shard_map/psum | solution.py:11
  385.1 201.0 %all-reduce.19.cloned.1.call-start = ((), (), s32[]{:S(2)}) async-start(), calls=%async_computation.5 | async-start | bytes 524288 | tf_op jit(solution)/shard_map/psum | solution.py:81
  548.2 2.2 slice-start.2
  550.4 11.8 %slice-start = ((s8[4456448]{0:T(1024)(128)(4,1)}), s8[262144]{0:T(1024)(128)(4,1)S(1)}, s32[]{:S(2)}) async-start(s8[4456448]{0:T(1024)(128)(4,1)} %bitcast.165), calls=%async_computation.7 | async-start | bytes 524288
  554.6 7.7 %slice-start.1 = ((s8[4456448]{0:T(1024)(128)(4,1)}), s8[4194304]{0:T(1024)(128)(4,1)S(1)}, s32[]{:S(2)}) async-start(s8[4456448]{0:T(1024)(128)(4,1)} %bitcast.165), calls=%async_computation.8 | async-start | bytes 8388608
  560.2 2.0 copy-start.4
Sparse Core Ops, SparseCore 0:
  9.7 35.0 all-reduce.20
  85.5 32.3 all-reduce.8
  127.6 163.0 all-reduce.10
  297.1 31.2 all-reduce.12
  345.7 31.3 all-reduce.14
  385.2 163.0 all-reduce.16
  554.7 31.2 all-reduce.18
where the time goes:
time: 616 us; the launch traced here: 608 us
  waiting for transfers between devices  427 us (69%)
  other arithmetic  73.2 us (12%)
  matrix products  47.7 us (8%)
  local copies, waits for them, and re-layouts  31.8 us (5%)
  between operations  14.3 us (2%)
  starting transfers between devices  13.6 us (2%)
    psum x3, waiting for transfers between devices, from_root(): return lax.psum(jnp.where(mine, array, jnp.zeros_like(array)), axis)  320 us
    psum x2, waiting for transfers between devices, per_device(): total = lax.psum(term, 'row')  59.2 us
    psum x2, waiting for transfers between devices, per_device(): summed = lax.psum(partial_sum, 'row')  47.1 us
    another operation x6, other arithmetic, right_solve(): return lax.linalg.triangular_solve(factor, rhs, left_side=False, lower=True)  41.1 us
    dot_general x4, matrix products, stacked_inner(): lax.dot_general(flat_left, flat_right, (((0,), (0,)), ((), ())), precisio...  17.4 us
    psum x2, starting transfers between devices, per_device(): summed = lax.psum(partial_sum, 'row')  13.4 us
  transfers between devices with their start and end apart: 7, of which 7 were waited for; matrix products, arithmetic and copies ran while one was open for 7% of the time, Pallas kernels for 0%

commit v1 on v0

--- a/solution.py
+++ b/solution.py
@@ -4,6 +4,14 @@
 from jax.sharding import PartitionSpec as P
 
 HIGH = lax.Precision.HIGHEST
+
+
+def add_in_pairs(shard, axis):
+    size, acc = (lax.axis_size(axis), shard)
+    for far in [1 << k for k in range(size.bit_length() - 1)]:
+        swap = [(i, i ^ far) for i in range(size)]
+        acc = acc + lax.ppermute(acc, axis, swap)
+    return acc
 
 
 def from_root(array, axis, root):
@@ -78,7 +86,7 @@
             cbar.reshape(-1, tile), row_factor, precision=HIGH, preferred_element_type=jnp.float32
         )
         partial_sum = stacked_inner(cbar, factor)
-        summed = lax.psum(partial_sum, "row")
+        summed = add_in_pairs(partial_sum, "row")
         own_row = grad[local] - (
             summed + jnp.dot(sym, row_factor, precision=HIGH, preferred_element_type=jnp.float32)
         )

time: 616 us -> 564 us (0.916)
  waiting for transfers between devices: 427 us -> 407 us
  matrix products: 47.7 us -> 36.7 us
  starting transfers between devices: 13.6 us -> 3.39 us
  other arithmetic: 73.2 us -> 65.1 us
    psum x2 -> x0, waiting for transfers between devices: 47.1 us -> none  [per_device(): summed = lax.psum(partial_sum, 'row')]
    ppermute x0 -> x4, waiting for transfers between devices: none -> 13.8 us  [add_in_pairs(): acc = acc + lax.ppermute(acc, axis, swap)]
    psum x2 -> x0, starting transfers between devices: 13.4 us -> none  [per_device(): summed = lax.psum(partial_sum, 'row')]
    psum x3, waiting for transfers between devices: 320 us -> 334 us  [from_root(): return lax.psum(jnp.where(mine, array, jnp.zeros_like(array)), axis)]
    dot_general x2, matrix products: 10.5 us -> 4.3 us  [per_device(): jnp.dot(cbar.reshape(-1, tile), row_factor, precision=HIGH, preferred_ele...]
  transfers between devices with their start and end apart: 7 -> 9, of which waited for: 7 -> 7; matrix products, arithmetic and copies ran while one was open for 7% -> 7% of each run, Pallas kernels for 0% -> 0%
where the time goes in v1:
time: 564 us; the launch traced here: 555 us
  waiting for transfers between devices  407 us (72%)
  other arithmetic  65.1 us (12%)
  matrix products  36.7 us (7%)
  local copies, waits for them, and re-layouts  28.7 us (5%)
  between operations  14 us (2%)
    psum x3, waiting for transfers between devices, from_root(): return lax.psum(jnp.where(mine, array, jnp.zeros_like(array)), axis)  334 us
    psum x2, waiting for transfers between devices, per_device(): total = lax.psum(term, 'row')  59 us
    another operation x6, other arithmetic, right_solve(): return lax.linalg.triangular_solve(factor, rhs, left_side=False, lower=True)  41.3 us
    dot_general x4, matrix products, stacked_inner(): lax.dot_general(flat_left, flat_right, (((0,), (0,)), ((), ())), precisio...  16.3 us
    ppermute x4, waiting for transfers between devices, add_in_pairs(): acc = acc + lax.ppermute(acc, axis, swap)  13.8 us
  transfers between devices with their start and end apart: 9, of which 7 were waited for; matrix products, arithmetic and copies ran while one was open for 7% of the time, Pallas kernels for 0%

profile of v1, /device:TPU:0, one launch (start us, length us, event | category | flops | bytes accessed | tf_op | source)
XLA Modules:
  0.0 554.8 jit_solution(11825394665499964062)
XLA Ops:
  6.5 1.6 select_bitcast_fusion.1
  8.4 4.3 convert_element_type.13
  12.6 32.2 %all-reduce.15.cloned.1.call-done = (bf16[256,256]{1,0:T(8,128)(2,1)}, bf16[256,256]{1,0:T(8,128)(2,1)}) async-done(((bf16[256,256]{1,0:T(8,128)(2,1)}, bf16[256,256]{1,0:T(8,128)(2,1)}), (bf16[256,256]{1,0:T(8,128)(2,1)}, bf16[256,256]{1,0:T(8,128)(2,1)})) %all-reduce.15.cloned.1.call-update) | async-done | bytes 262160 | tf_op jit(solution)/shard_map/psum | solution.py:19
  44.8 1.0 fusion.25
  45.9 3.8 while.14
  46.0 0.6 fusion.114
  46.5 1.3 bitcast_dynamic-update-slice_fusion.4
  47.9 0.6 fusion.114
  48.5 1.3 bitcast_dynamic-update-slice_fusion.4
  49.8 19.7 %custom-call.10 = f32[2,128,128]{1,2,0:T(8,128)S(1)} custom-call(f32[2,128,128]{2,1,0:T(8,128)S(1)} %get-tuple-element.71), custom_call_target="InvertDiagBlocksLowerTriangular" | custom-call | tf_op jit(solution)/shard_map/triangular_solve/custom-call.1 | solution.py:23
  69.5 0.3 fusion.60
  69.8 0.4 convolution_subtract_fusion.7
  70.2 0.3 fusion.64
  70.4 3.9 convolution_bitcast_fusion
  74.3 5.7 %copy.9 = f32[4096,256]{1,0:T(8,128)} copy(f32[4096,256]{0,1:T(8,128)} %convolution_bitcast_fusion) | data formatting | bytes 8388608 | tf_op jit(solution)/shard_map/reshape | solution.py:52
  80.1 5.1 fusion.5
  85.2 4.7 broadcast_select_fusion
  89.9 27.6 %all-reduce.7.cloned.1.call-done = f32[256,256]{1,0:T(8,128)} async-done(((f32[256,256]{1,0:T(8,128)}), f32[256,256]{1,0:T(8,128)}) %all-reduce.7.cloned.1.call-update) | async-done | bytes 262160 | tf_op jit(solution)/shard_map/psum | solution.py:79
  117.6 1.3 fusion.33
  118.8 0.3 fusion.52
  119.1 0.3 convolution_subtract_fusion.6
  119.7 0.3 fusion.50
  120.0 0.4 convolution_subtract_fusion.5
  120.4 0.3 fusion.62
  120.7 0.7 pad_maximum_fusion
  121.4 1.1 copy.4
  122.5 4.7 maximum_select_fusion
  127.3 3.8 while.15
  127.3 0.6 fusion.115
  127.9 1.3 bitcast_dynamic-update-slice_fusion.5
  129.2 0.6 fusion.115
  129.8 1.3 bitcast_dynamic-update-slice_fusion.5
  131.1 19.8 %custom-call.13 = f32[2,128,128]{1,2,0:T(8,128)S(1)} custom-call(f32[2,128,128]{2,1,0:T(8,128)S(1)} %get-tuple-element.74), custom_call_target="InvertDiagBlocksLowerTriangular" | custom-call | tf_op jit(solution)/shard_map/triangular_solve/custom-call.1 | solution.py:23
  151.0 0.3 fusion.58
  151.2 0.4 convolution_subtract_fusion.4
  151.6 0.3 fusion.67
  151.9 138.5 %all-reduce.9.cloned.1.call-done = f32[17,256,256]{2,1,0:T(8,128)} async-done(((f32[17,256,256]{2,1,0:T(8,128)}), f32[17,256,256]{2,1,0:T(8,128)}) %all-reduce.9.cloned.1.call-update) | async-done | bytes 4456464 | tf_op jit(solution)/shard_map/psum | solution.py:19
  290.4 2.6 slice-done.1
  292.9 3.4 fusion.83
  296.5 2.0 bitcast_subtract_fusion
  298.6 1.5 collective-permute-start.1
  300.1 0.3 fusion.22
  300.4 6.9 %collective-permute-done.1 = f32[256,256]{1,0:T(8,128)S(1)} collective-permute-done((f32[256,256]{1,0:T(8,128)S(1)}, f32[256,256]{1,0:T(8,128)S(1)}, u32[]{:S(2)}, u32[]{:S(2)}) %collective-permute-start.1) | collective-permute-done | bytes 262176 | tf_op jit(solution)/shard_map/ppermute | solution.py:13
  307.3 1.1 fusion.13
  308.4 1.2 fusion
  309.6 3.7 convolution_select_fusion
  313.4 2.0 copy-done.4
  315.4 4.4 convolution_subtract_fusion.1
  319.9 31.4 %all-reduce.11.cloned.1.call-done = f32[256,256]{1,0:T(8,128)} async-done(((f32[256,256]{1,0:T(8,128)}), f32[256,256]{1,0:T(8,128)}) %all-reduce.11.cloned.1.call-update) | async-done | bytes 262160 | tf_op jit(solution)/shard_map/psum | solution.py:79
  351.2 1.3 fusion.36
  352.8 0.3 convolution_subtract_fusion.3
  353.4 0.3 fusion.46
  353.6 0.4 convolution_subtract_fusion.2
  354.0 0.3 fusion.65
  354.5 4.7 maximum_select_fusion.1
  359.2 163.1 %all-reduce.13.cloned.1.call-done = f32[17,256,256]{2,1,0:T(8,128)} async-done(((f32[17,256,256]{2,1,0:T(8,128)}), f32[17,256,256]{2,1,0:T(8,128)}) %all-reduce.13.cloned.1.call-update) | async-done | bytes 4456464 | tf_op jit(solution)/shard_map/psum | solution.py:19
  522.4 3.1 slice-done
  525.5 3.5 fusion.84
  529.1 2.3 convolution_subtract_fusion
  531.4 1.5 collective-permute-start.3
  533.0 0.3 fusion.19
  533.2 6.9 %collective-permute-done.3 = f32[256,256]{1,0:T(8,128)S(1)} collective-permute-done((f32[256,256]{1,0:T(8,128)S(1)}, f32[256,256]{1,0:T(8,128)S(1)}, u32[]{:S(2)}, u32[]{:S(2)}) %collective-permute-start.3) | collective-permute-done | bytes 262176 | tf_op jit(solution)/shard_map/ppermute | solution.py:13
  540.3 1.2 select_bitcast_fusion
  541.5 6.3 %copy.7 = f32[16,1,256,1,256]{4,3,2,1,0:T(1,128)} copy(f32[16,1,256,1,256]{4,2,0,3,1:T(8,128)S(1)} %select_bitcast_fusion) | data formatting | bytes 8388608 | tf_op jit(solution)/shard_map/reshape | solution.py:102
  (62 shorter events, 2.0 us)
Async XLA Ops:
  6.5 38.3 %all-reduce.15.cloned.1.call-start = ((), (), s32[]{:S(2)}) async-start(), calls=%async_computation.4 | async-start | bytes 524288 | tf_op jit(solution)/shard_map/psum | solution.py:19
  8.2 109.4 %all-reduce.7.cloned.1.call-start = ((), (), s32[]{:S(2)}) async-start(), calls=%async_computation | async-start | bytes 524288 | tf_op jit(solution)/shard_map/psum | solution.py:79
  8.3 62.1 %copy-start.6 = (bf16[16,1,256,1,256]{4,2,3,1,0:T(8,128)(2,1)S(1)}, bf16[16,1,256,1,256]{4,2,3,1,0:T(8,128)(2,1)}, u32[]{:S(2)}) copy-start(bf16[16,1,256,1,256]{4,2,3,1,0:T(8,128)(2,1)} %param.11) | copy-start | bytes 6291460
  74.3 5.8 %copy-start.5 = (bf16[16,1,256,1,256]{4,2,3,1,0:T(8,128)(2,1)S(1)}, bf16[16,1,256,1,256]{4,2,3,1,0:T(8,128)(2,1)}, u32[]{:S(2)}) copy-start(bf16[16,1,256,1,256]{4,2,3,1,0:T(8,128)(2,1)} %param.10) | copy-start | bytes 6291460
  85.1 205.3 %all-reduce.9.cloned.1.call-start = ((), (), s32[]{:S(2)}) async-start(), calls=%async_computation.1 | async-start | bytes 8912896 | tf_op jit(solution)/shard_map/psum | solution.py:19
  85.2 32.4 %copy-start.9 = (bf16[256,256]{1,0:T(8,128)(2,1)S(1)}, bf16[256,256]{1,0:T(8,128)(2,1)}, u32[]{:S(2)}) copy-start(bf16[256,256]{1,0:T(8,128)(2,1)} %get-tuple-element.93) | copy-start | bytes 393220
  127.2 224.0 %all-reduce.11.cloned.1.call-start = ((), (), s32[]{:S(2)}) async-start(), calls=%async_computation.2 | async-start | bytes 524288 | tf_op jit(solution)/shard_map/psum | solution.py:79
  290.4 2.6 slice-start.1
  290.4 6.1 %copy-start.3 = (f32[17,256,256]{2,1,0:T(8,128)S(1)}, f32[17,256,256]{2,1,0:T(8,128)}, u32[]{:S(2)}) copy-start(f32[17,256,256]{2,1,0:T(8,128)} %all-reduce.9.cloned.1.call-done) | copy-start | bytes 13369348
  290.4 6.1 %copy-start.7 = (bf16[16,1,256,1,256]{4,2,3,1,0:T(8,128)(2,1)S(1)}, bf16[16,1,256,1,256]{4,2,3,1,0:T(8,128)(2,1)}, u32[]{:S(2)}) copy-start(bf16[16,1,256,1,256]{4,2,3,1,0:T(8,128)(2,1)} %param.11) | copy-start | bytes 6291460
  296.4 2.1 collective-permute-start
  298.6 8.8 %collective-permute-start.1 = (f32[256,256]{1,0:T(8,128)S(1)}, f32[256,256]{1,0:T(8,128)S(1)}, u32[]{:S(2)}, u32[]{:S(2)}) collective-permute-start(f32[256,256]{1,0:T(8,128)S(1)} %add.66), channel_id=1, source_target_pairs={{0,16},{8,24},{16,0},{24,8},{1,17},{9,25},{17,1},{25,9},{2,18},{10... | collective-permute-start | bytes 786440 | tf_op jit(solution)/shard_map/ppermute | solution.py:13
  309.6 3.8 copy-start
  313.4 2.0 copy-start.4
  313.4 37.9 %copy-start.8 = (bf16[256,256]{1,0:T(8,128)(2,1)S(1)}, bf16[256,256]{1,0:T(8,128)(2,1)}, u32[]{:S(2)}) copy-start(bf16[256,256]{1,0:T(8,128)(2,1)} %get-tuple-element.94) | copy-start | bytes 393220
  319.8 202.6 %all-reduce.13.cloned.1.call-start = ((), (), s32[]{:S(2)}) async-start(), calls=%async_computation.3 | async-start | bytes 8912896 | tf_op jit(solution)/shard_map/psum | solution.py:19
  522.4 3.1 slice-start
  522.4 6.7 %copy-start.2 = (f32[17,256,256]{2,1,0:T(8,128)S(1)}, f32[17,256,256]{2,1,0:T(8,128)}, u32[]{:S(2)}) copy-start(f32[17,256,256]{2,1,0:T(8,128)} %all-reduce.13.cloned.1.call-done) | copy-start | bytes 13369348
  522.4 6.7 %copy-start.1 = (f32[16,256,256]{2,1,0:T(8,128)S(1)}, f32[16,256,256]{2,1,0:T(8,128)}, u32[]{:S(2)}) copy-start(f32[16,256,256]{2,1,0:T(8,128)} %copy-done) | copy-start | bytes 12582916
  529.0 2.4 collective-permute-start.2
  531.4 8.8 %collective-permute-start.3 = (f32[256,256]{1,0:T(8,128)S(1)}, f32[256,256]{1,0:T(8,128)S(1)}, u32[]{:S(2)}, u32[]{:S(2)}) collective-permute-start(f32[256,256]{1,0:T(8,128)S(1)} %add.70), channel_id=1, source_target_pairs={{0,16},{8,24},{16,0},{24,8},{1,17},{9,25},{17,1},{25,9},{2,18},{10... | collective-permute-start | bytes 786440 | tf_op jit(solution)/shard_map/ppermute | solution.py:13
Sparse Core Ops, SparseCore 0:
  9.7 35.0 all-reduce.14
  85.2 32.2 all-reduce.6
  127.3 163.0 all-reduce.8
  319.9 31.2 all-reduce.10
  359.3 162.9 all-reduce.12
